TPU v7x, 32 devices: a whole 2x2x4 slice. The times are simulated.
32 devices in a mesh: rows: 4 (over z), tp: 4 (over y, x), unit: 2 (over core).
Axes of the slice: x: 2, y: 2, z: 4, core: 2. Of those that a mesh axis runs over, the one named last changes fastest.
Arguments:
- w_query: bfloat16 [5120, 4096], P(('unit', 'rows'), 'tp'), parts along dimension 0, may hold values from -0.125 to 0.125
- low_query: bfloat16 [5120, 64], P(('unit', 'rows')), parts along dimension 0, may hold values from -0.125 to 0.125
- high_query: bfloat16 [128, 4096], P('unit', 'tp'), parts along dimension 0, may hold values from -0.75 to 0.75
- w_key: bfloat16 [5120, 1024], P(('unit', 'rows'), 'tp'), parts along dimension 0, may hold values from -0.125 to 0.125
- low_key: bfloat16 [5120, 64], P(('unit', 'rows')), parts along dimension 0, may hold values from -0.125 to 0.125
- high_key: bfloat16 [128, 1024], P('unit', 'tp'), parts along dimension 0, may hold values from -0.75 to 0.75
- w_value: bfloat16 [5120, 1024], P(('unit', 'rows'), 'tp'), parts along dimension 0, may hold values from -0.125 to 0.125
- low_value: bfloat16 [5120, 64], P(('unit', 'rows')), parts along dimension 0, may hold values from -0.125 to 0.125
- high_value: bfloat16 [128, 1024], P('unit', 'tp'), parts along dimension 0, may hold values from -0.75 to 0.75
- w_mixed: bfloat16 [8192, 2560], P(('unit', 'tp'), 'rows'), parts along dimension 0, may hold values from -0.09375 to 0.09375
- low_mixed: bfloat16 [8192, 64], P(('unit', 'tp')), parts along dimension 0, may hold values from -0.09375 to 0.09375
- high_mixed: bfloat16 [128, 2560], P('unit', 'rows'), parts along dimension 0, may hold values from -0.75 to 0.75
- norm_train: float32 [5120], P(('unit', 'rows', 'tp')), parts along dimension 0, may hold values from 0.25 to 1.75
- norm_step: float32 [5120], P(('unit', 'rows', 'tp')), parts along dimension 0, may hold values from -0.3 to 0.3
Outputs:
- final_query: bfloat16 [5120, 4096], P('unit', 'tp'), parts along dimension 0
- final_key: bfloat16 [5120, 1024], P('unit', 'tp'), parts along dimension 0
- final_value: bfloat16 [5120, 1024], P('unit', 'tp'), parts along dimension 0
- final_mixed: bfloat16 [8192, 2560], P(('unit', 'tp')), parts along dimension 0
- serve_norm: bfloat16 [5120], P('unit'), parts along dimension 0
There are 2 independent parts, one for each index of `unit`. A program takes and returns all parts, laid end to end along the dimension named above; each array names one. Nothing has to cross between parts.
All inputs are finite; a program needn't handle non-finite values.
Results may differ from a plain program's by a relative error of at most 0.001.
Values may be sent and summed in bfloat16 or wider, within the bound.
A program may use at most 128 MiB of HBM per device.

v0:
```python
import jax
import jax.numpy as jnp
from jax import lax
from jax.sharding import PartitionSpec as P

mix_rate = 0.5


def shards(
    w_query,
    low_query,
    high_query,
    w_key,
    low_key,
    high_key,
    w_value,
    low_value,
    high_value,
    w_mixed,
    low_mixed,
    high_mixed,
    norm_train,
    norm_step,
):
    result_query = w_query.astype(jnp.float32) + mix_rate * jnp.dot(
        low_query, high_query, preferred_element_type=jnp.float32
    )
    result_key = w_key.astype(jnp.float32) + mix_rate * jnp.dot(
        low_key, high_key, preferred_element_type=jnp.float32
    )
    result_value = w_value.astype(jnp.float32) + mix_rate * jnp.dot(
        low_value, high_value, preferred_element_type=jnp.float32
    )
    result_mixed = w_mixed.astype(jnp.float32) + mix_rate * jnp.dot(
        low_mixed, high_mixed, preferred_element_type=jnp.float32
    )
    narrow_query, narrow_key, narrow_value, narrow_mixed = (
        result_query.astype(jnp.bfloat16),
        result_key.astype(jnp.bfloat16),
        result_value.astype(jnp.bfloat16),
        result_mixed.astype(jnp.bfloat16),
    )
    final_query, final_key, final_value, final_mixed = (
        lax.all_gather(narrow_query, "rows", axis=0, tiled=True),
        lax.all_gather(narrow_key, "rows", axis=0, tiled=True),
        lax.all_gather(narrow_value, "rows", axis=0, tiled=True),
        lax.all_gather(narrow_mixed, "rows", axis=1, tiled=True),
    )
    serve_norm = lax.all_gather(
        (norm_train + norm_step).astype(jnp.bfloat16), ("rows", "tp"), axis=0, tiled=True
    )
    return (final_query, final_key, final_value, final_mixed, serve_norm)


def solution(mesh):
    return jax.shard_map(
        shards,
        mesh=mesh,
        in_specs=(
            P(("unit", "rows"), "tp"),
            P(("unit", "rows"), None),
            P("unit", "tp"),
            P(("unit", "rows"), "tp"),
            P(("unit", "rows"), None),
            P("unit", "tp"),
            P(("unit", "rows"), "tp"),
            P(("unit", "rows"), None),
            P("unit", "tp"),
            P(("unit", "tp"), "rows"),
            P(("unit", "tp"), None),
            P("unit", "rows"),
            P(("unit", "rows", "tp")),
            P(("unit", "rows", "tp")),
        ),
        out_specs=(
            P("unit", "tp"),
            P("unit", "tp"),
            P("unit", "tp"),
            P(("unit", "tp"), None),
            P("unit"),
        ),
        check_vma=False,
    )
```

profile of v0, /device:TPU:0, one launch (start us, length us, event | category | flops | bytes accessed | tf_op | source)
XLA Modules:
  0.0 295.5 jit_solution(12324406735975937253)
XLA Ops:
  7.2 0.0 copy-start
  7.2 0.0 copy-start.2
  7.2 0.0 all-gather.7.cloned.1.call-start
  7.2 2.1 fusion.2
  9.4 0.0 all-gather.7.cloned.1.call-update
  9.4 0.0 copy-start.3
  9.4 0.0 copy-start.6
  9.4 0.0 copy-start.7
  9.4 0.0 all-gather.9.cloned.1.call-start
  9.5 2.1 fusion.3
  11.6 0.0 all-gather.9.cloned.1.call-update
  11.7 0.0 all-gather.5.cloned.1.call-start
  11.7 0.0 copy-done
  11.7 0.0 copy-done.2
  11.7 2.5 add_convert_fusion.1
  14.2 0.0 all-gather.5.cloned.1.call-update
  14.2 0.0 all-gather.11.cloned.1.call-start
  14.3 0.0 copy-done.3
  14.3 1.6 add_convert_fusion
  15.9 0.0 all-gather.11.cloned.1.call-update
  15.9 0.6 dynamic-slice
  17.2 0.2 dynamic-update-slice
  17.5 46.0 %all-reduce = bf16[2560]{0:T(1024)(128)(2,1)} all-reduce(bf16[2560]{0:T(1024)(128)(2,1)S(1)} %dynamic-update-slice), channel_id=1, replica_groups=mesh['rows'=4,'tp'=4,'unit'=2] {'rows','tp'}, use_global_device_ids=true, to_apply=%add | all-reduce | flops 2560 | bytes 10240
  63.5 16.7 %all-gather.9.cloned.1.call-done = bf16[2560,256]{1,0:T(8,128)(2,1)} async-done(((bf16[640,256]{1,0:T(8,128)(2,1)}), bf16[2560,256]{1,0:T(8,128)(2,1)}) %all-gather.9.cloned.1.call-update) | async-done | bytes 1310736 | tf_op jit(solution)/shard_map/all_gather | solution.py:46
  80.3 99.4 %all-gather.5.cloned.1.call-done = bf16[2560,1024]{1,0:T(8,128)(2,1)} async-done(((bf16[640,1024]{1,0:T(8,128)(2,1)}), bf16[2560,1024]{1,0:T(8,128)(2,1)}) %all-gather.5.cloned.1.call-update) | async-done | bytes 5242896 | tf_op jit(solution)/shard_map/all_gather | solution.py:44
  179.7 98.4 %all-gather.11.cloned.1.call-done = bf16[1024,2560]{1,0:T(8,128)(2,1)} async-done(((bf16[1024,640]{1,0:T(8,128)(2,1)}), bf16[1024,2560]{1,0:T(8,128)(2,1)}) %all-gather.11.cloned.1.call-update) | async-done | bytes 5242896 | tf_op jit(solution)/shard_map/all_gather | solution.py:47
  278.1 5.6 %copy.24 = bf16[2560,1024]{1,0:T(8,128)(2,1)} copy(bf16[2560,1024]{1,0:T(8,128)(2,1)} %all-gather.5.cloned.1.call-done) | data formatting | bytes 10485760
  283.7 0.0 copy-done.4
  283.7 1.1 copy.25
  284.8 0.7 copy-done.5
  285.5 1.1 copy.26
  286.6 2.4 copy.27
  (15 shorter events, 0.0 us)
Async XLA Ops:
  7.2 4.5 %copy-start = (bf16[64,1024]{1,0:T(8,128)(2,1)S(1)}, bf16[64,1024]{1,0:T(8,128)(2,1)}, u32[]{:S(2)}) copy-start(bf16[64,1024]{1,0:T(8,128)(2,1)} %param.16) | copy-start | bytes 393220
  7.2 4.5 %copy-start.2 = (bf16[640,1024]{1,0:T(8,128)(2,1)S(1)}, bf16[640,1024]{1,0:T(8,128)(2,1)}, u32[]{:S(2)}) copy-start(bf16[640,1024]{1,0:T(8,128)(2,1)} %param.14) | copy-start | bytes 3932164
  7.2 56.3 %all-gather.7.cloned.1.call-start = ((), (), s32[]{:S(2)}) async-start(), calls=%async_computation.1 | async-start | bytes 1638400 | tf_op jit(solution)/shard_map/all_gather | solution.py:45
  9.4 4.9 %copy-start.3 = (bf16[1024,640]{1,0:T(8,128)(2,1)S(1)}, bf16[1024,640]{1,0:T(8,128)(2,1)}, u32[]{:S(2)}) copy-start(bf16[1024,640]{1,0:T(8,128)(2,1)} %param.23) | copy-start | bytes 3932164
  9.4 4.9 %copy-start.6 = (bf16[1024,64]{0,1:T(8,128)(2,1)S(1)}, bf16[1024,64]{0,1:T(8,128)(2,1)}, u32[]{:S(2)}) copy-start(bf16[1024,64]{0,1:T(8,128)(2,1)} %param.24) | copy-start | bytes 393220
  9.4 4.9 %copy-start.7 = (bf16[64,640]{1,0:T(8,128)(2,1)S(1)}, bf16[64,640]{1,0:T(8,128)(2,1)}, u32[]{:S(2)}) copy-start(bf16[64,640]{1,0:T(8,128)(2,1)} %param.25) | copy-start | bytes 245764
  9.4 70.8 %all-gather.9.cloned.1.call-start = ((), (), s32[]{:S(2)}) async-start(), calls=%async_computation.2 | async-start | bytes 1638400 | tf_op jit(solution)/shard_map/all_gather | solution.py:46
  11.7 168.0 %all-gather.5.cloned.1.call-start = ((), (), s32[]{:S(2)}) async-start(), calls=%async_computation | async-start | bytes 6553600 | tf_op jit(solution)/shard_map/all_gather | solution.py:44
  14.2 1.7 copy-start.10
  14.2 3.0 %copy-start.8 = (f32[160]{0:T(256)S(1)}, f32[160]{0:T(256)}, u32[]{:S(2)}) copy-start(f32[160]{0:T(256)} %param.26) | copy-start | bytes 1924
  14.2 3.0 %copy-start.9 = (f32[160]{0:T(256)S(1)}, f32[160]{0:T(256)}, u32[]{:S(2)}) copy-start(f32[160]{0:T(256)} %param.27) | copy-start | bytes 1924
  14.2 263.9 %all-gather.11.cloned.1.call-start = ((), (), s32[]{:S(2)}) async-start(), calls=%async_computation.3 | async-start | bytes 6553600 | tf_op jit(solution)/shard_map/all_gather | solution.py:47
  63.5 220.2 %copy-start.4 = (bf16[2560,256]{1,0:T(8,128)(2,1)S(1)}, bf16[2560,256]{1,0:T(8,128)(2,1)}, u32[]{:S(2)}) copy-start(bf16[2560,256]{1,0:T(8,128)(2,1)} %all-gather.7.cloned.1.call-done) | copy-start | bytes 3932164
  278.1 8.5 %copy-start.1 = (bf16[1024,2560]{1,0:T(8,128)(2,1)S(1)}, bf16[1024,2560]{1,0:T(8,128)(2,1)}, u32[]{:S(2)}) copy-start(bf16[1024,2560]{1,0:T(8,128)(2,1)} %all-gather.11.cloned.1.call-done) | copy-start | bytes 15728644
  283.7 1.8 copy-start.5
Sparse Core Ops, SparseCore 0:
  10.1 36.3 all-gather.6
  48.7 31.4 all-gather.8
  82.4 97.2 all-gather.4
  181.7 96.3 all-gather.10
where the time goes:
time: 296 us; the launch traced here: 295 us
  waiting for transfers between devices  215 us (73%)
  blocking collectives  46 us (16%)
  between operations  14.5 us (5%)
  local copies, waits for them, and re-layouts  11.7 us (4%)
  matrix products  8.35 us (3%)
    all_gather x1, waiting for transfers between devices, shards(): lax.all_gather(narrow_query, 'rows', axis=0, tiled=True)  99.4 us
    all_gather x1, waiting for transfers between devices, shards(): lax.all_gather(narrow_mixed, 'rows', axis=1, tiled=True)  98.4 us
    unnamed x1, blocking collectives  46 us
    all_gather x1, waiting for transfers between devices, shards(): lax.all_gather(narrow_value, 'rows', axis=0, tiled=True)  16.7 us
    unnamed x29, local copies, waits for them, and re-layouts  11.7 us
  transfers between devices with their start and end apart: 4, of which 3 were waited for; matrix products, arithmetic and copies ran while one was open for 2% of the time, Pallas kernels for 0%

commit v1 on v0

--- a/solution.py
+++ b/solution.py
@@ -4,6 +4,13 @@
 from jax.sharding import PartitionSpec as P
 
 mix_rate = 0.5
+
+
+def _advance_clusters(tile_in):
+    opened = jnp.concatenate(
+        lax.all_to_all(jnp.stack([tile_in] * lax.axis_size("rows")), "rows", 0, 0), axis=1
+    )
+    return opened
 
 
 def shards(
@@ -44,7 +51,7 @@
         lax.all_gather(narrow_query, "rows", axis=0, tiled=True),
         lax.all_gather(narrow_key, "rows", axis=0, tiled=True),
         lax.all_gather(narrow_value, "rows", axis=0, tiled=True),
-        lax.all_gather(narrow_mixed, "rows", axis=1, tiled=True),
+        _advance_clusters(narrow_mixed),
     )
     serve_norm = lax.all_gather(
         (norm_train + norm_step).astype(jnp.bfloat16), ("rows", "tp"), axis=0, tiled=True

time: 296 us -> 280 us (0.946)
  waiting for transfers between devices: 215 us -> 57.2 us
  blocking collectives: 46 us -> 166 us
  local copies, waits for them, and re-layouts: 11.7 us -> 27.7 us
  starting transfers between devices: 0.16 us -> 6.6 us
    unnamed x1, blocking collectives: 46 us -> 166 us
    all_gather x1 -> x0, waiting for transfers between devices: 98.4 us -> none  [shards(): lax.all_gather(narrow_mixed, 'rows', axis=1, tiled=True)]
    all_gather x1, waiting for transfers between devices: 99.4 us -> 57.2 us  [shards(): lax.all_gather(narrow_query, 'rows', axis=0, tiled=True)]
    all_gather x1, waiting for transfers between devices: 16.7 us -> 0.01 us  [shards(): lax.all_gather(narrow_value, 'rows', axis=0, tiled=True)]
    all_to_all x0 -> x1, local copies, waits for them, and re-layouts: none -> 7.87 us  [_advance_clusters(): lax.all_to_all(jnp.stack([tile_in] * lax.axis_size('rows')), 'rows', 0, 0)]
    all_to_all x0 -> x1, starting transfers between devices: none -> 6.48 us  [_advance_clusters(): lax.all_to_all(jnp.stack([tile_in] * lax.axis_size('rows')), 'rows', 0, 0)]
    unnamed x29 -> x25, local copies, waits for them, and re-layouts: 11.7 us -> 17.1 us
  transfers between devices with their start and end apart: 4 -> 4, of which waited for: 3 -> 1; matrix products, arithmetic and copies ran while one was open for 2% -> 9% of each run, Pallas kernels for 0% -> 0%
where the time goes in v1:
time: 280 us
  blocking collectives  166 us (59%)
  waiting for transfers between devices  57.2 us (20%)
  local copies, waits for them, and re-layouts  27.7 us (10%)
  between operations  14.5 us (5%)
  matrix products  7.59 us (3%)
  starting transfers between devices  6.6 us (2%)
    unnamed x1, blocking collectives  166 us
    all_gather x1, waiting for transfers between devices, shards(): lax.all_gather(narrow_query, 'rows', axis=0, tiled=True)  57.2 us
    unnamed x25, local copies, waits for them, and re-layouts  17.1 us
    all_to_all x1, local copies, waits for them, and re-layouts, _advance_clusters(): lax.all_to_all(jnp.stack([tile_in] * lax.axis_size('rows')), 'rows', 0, 0)  7.87 us
    all_to_all x1, starting transfers between devices, _advance_clusters(): lax.all_to_all(jnp.stack([tile_in] * lax.axis_size('rows')), 'rows', 0, 0)  6.48 us
  transfers between devices with their start and end apart: 4, of which 1 were waited for; matrix products, arithmetic and copies ran while one was open for 9% of the time, Pallas kernels for 0%

profile of v1, /device:TPU:0, one launch (start us, length us, event | category | flops | bytes accessed | tf_op | source)
XLA Modules:
  0.0 279.7 jit_solution(3286545281461018136)
XLA Ops:
  7.2 0.0 copy-start
  7.2 0.0 all-gather.6.cloned.1.call-start
  7.2 2.1 fusion.2
  9.3 0.0 all-gather.6.cloned.1.call-update
  9.3 0.0 all-gather.8.cloned.1.call-start
  9.4 2.0 fusion.3
  11.4 0.0 all-gather.8.cloned.1.call-update
  11.4 0.0 copy-done
  11.4 1.9 add_convert_fusion
  13.4 2.8 stack.2
  16.1 6.5 %all-to-all-start = ((bf16[4,1024,640]{2,1,0:T(8,128)(2,1)}), bf16[4,1024,640]{2,1,0:T(8,128)(2,1)}, u32[]{:S(2)}, u32[]{:S(2)}) async-start(bf16[4,1024,640]{2,1,0:T(8,128)(2,1)} %stack.2), calls=%async_computation | async-start | bytes 10485760 | tf_op jit(solution)/shard_map/all_to_all | solution.py:11
  22.6 0.0 all-gather.4.cloned.1.call-start
  22.7 0.0 copy-done.1
  22.7 0.0 copy-done.4
  22.7 0.0 copy-done.5
  22.7 1.6 add_convert_fusion.1
  24.3 0.0 all-gather.4.cloned.1.call-update
  24.3 0.0 copy-done.8
  24.3 0.6 dynamic-slice
  25.6 0.0 copy-done.6
  25.6 0.0 copy-done.7
  25.6 0.2 dynamic-update-slice
  25.8 166.1 %all-reduce = bf16[2560]{0:T(1024)(128)(2,1)} all-reduce(bf16[2560]{0:T(1024)(128)(2,1)S(1)} %dynamic-update-slice), channel_id=1, replica_groups=mesh['rows'=4,'tp'=4,'unit'=2] {'rows','tp'}, use_global_device_ids=true, to_apply=%add | all-reduce | flops 2560 | bytes 10240
  192.0 0.0 all-to-all-done
  192.0 7.9 %copy.19 = bf16[4,1024,640]{1,2,0:T(8,128)(2,1)} copy(bf16[4,1024,640]{2,1,0:T(8,128)(2,1)} %all-to-all-done) | data formatting | bytes 10485760 | tf_op jit(solution)/shard_map/all_to_all | solution.py:11
  199.8 7.9 %copy.20 = bf16[1024,2560]{1,0:T(8,128)(2,1)} copy(bf16[1024,2560]{0,1:T(8,128)(2,1)} %bitcast.12) | data formatting | bytes 10485760
  207.8 57.2 %all-gather.4.cloned.1.call-done = bf16[2560,1024]{1,0:T(8,128)(2,1)} async-done(((bf16[640,1024]{1,0:T(8,128)(2,1)}), bf16[2560,1024]{1,0:T(8,128)(2,1)}) %all-gather.4.cloned.1.call-update) | async-done | bytes 5242896 | tf_op jit(solution)/shard_map/all_gather | solution.py:51
  264.9 5.4 %copy.25 = bf16[2560,1024]{1,0:T(8,128)(2,1)} copy(bf16[2560,1024]{1,0:T(8,128)(2,1)} %all-gather.4.cloned.1.call-done) | data formatting | bytes 10485760
  270.4 0.0 copy-done.2
  270.4 1.1 copy.26
  271.4 0.7 copy-done.3
  272.2 1.1 copy.27
  (12 shorter events, 0.0 us)
Async XLA Ops:
  7.2 4.3 %copy-start = (bf16[1024,64]{0,1:T(8,128)(2,1)S(1)}, bf16[1024,64]{0,1:T(8,128)(2,1)}, u32[]{:S(2)}) copy-start(bf16[1024,64]{0,1:T(8,128)(2,1)} %param.24) | copy-start | bytes 393220
  7.2 184.8 %all-gather.6.cloned.1.call-start = ((), (), s32[]{:S(2)}) async-start(), calls=%async_computation.2 | async-start | bytes 1638400 | tf_op jit(solution)/shard_map/all_gather | solution.py:52
  9.3 182.7 %all-gather.8.cloned.1.call-start = ((), (), s32[]{:S(2)}) async-start(), calls=%async_computation.3 | async-start | bytes 1638400 | tf_op jit(solution)/shard_map/all_gather | solution.py:53
  16.1 6.5 %copy-start.1 = (bf16[640,1024]{1,0:T(8,128)(2,1)S(1)}, bf16[640,1024]{1,0:T(8,128)(2,1)}, u32[]{:S(2)}) copy-start(bf16[640,1024]{1,0:T(8,128)(2,1)} %param.14) | copy-start | bytes 3932164
  16.1 6.6 %copy-start.4 = (bf16[64,1024]{1,0:T(8,128)(2,1)S(1)}, bf16[64,1024]{1,0:T(8,128)(2,1)}, u32[]{:S(2)}) copy-start(bf16[64,1024]{1,0:T(8,128)(2,1)} %param.16) | copy-start | bytes 393220
  16.1 6.6 %copy-start.5 = (bf16[640,64]{0,1:T(8,128)(2,1)S(1)}, bf16[640,64]{0,1:T(8,128)(2,1)}, u32[]{:S(2)}) copy-start(bf16[640,64]{0,1:T(8,128)(2,1)} %param.15) | copy-start | bytes 245764
  16.1 175.9 %all-to-all-start = ((bf16[4,1024,640]{2,1,0:T(8,128)(2,1)}), bf16[4,1024,640]{2,1,0:T(8,128)(2,1)}, u32[]{:S(2)}, u32[]{:S(2)}) async-start(bf16[4,1024,640]{2,1,0:T(8,128)(2,1)} %stack.2), calls=%async_computation | async-start | bytes 10485760 | tf_op jit(solution)/shard_map/all_to_all | solution.py:11
  22.6 1.7 copy-start.8
  22.6 2.9 %copy-start.6 = (f32[160]{0:T(256)S(1)}, f32[160]{0:T(256)}, u32[]{:S(2)}) copy-start(f32[160]{0:T(256)} %param.26) | copy-start | bytes 1924
  22.6 3.0 %copy-start.7 = (f32[160]{0:T(256)S(1)}, f32[160]{0:T(256)}, u32[]{:S(2)}) copy-start(f32[160]{0:T(256)} %param.27) | copy-start | bytes 1924
  22.6 242.3 %all-gather.4.cloned.1.call-start = ((), (), s32[]{:S(2)}) async-start(), calls=%async_computation.1 | async-start | bytes 6553600 | tf_op jit(solution)/shard_map/all_gather | solution.py:51
  207.8 62.6 %copy-start.2 = (bf16[2560,256]{1,0:T(8,128)(2,1)S(1)}, bf16[2560,256]{1,0:T(8,128)(2,1)}, u32[]{:S(2)}) copy-start(bf16[2560,256]{1,0:T(8,128)(2,1)} %all-gather.6.cloned.1.call-done) | copy-start | bytes 3932164
  270.4 1.8 copy-start.3
Sparse Core Ops, SparseCore 0:
  10.1 72.9 all-gather.5
  85.3 68.6 all-gather.7
  156.2 108.7 all-gather.3
